TPU v7x, 32 devices: a whole 2x2x4 slice. The times are simulated.
32 devices in a mesh: dp: 8 (over y, x, core), mp: 4 (over z).
Axes of the slice: x: 2, y: 2, z: 4, core: 2. Of those that a mesh axis runs over, the one named last changes fastest.
Arguments:
- tokens: bfloat16 [8192, 2048], P('dp'), may hold values from -6 to 6
- doc_ids: int32 [16, 512], P('dp'), may hold values from 0 to 3, never falling along the last dimension, each value on 1 to 256 neighbouring positions
- selection: int32 [16, 512], P('dp'), may hold values 0 or 1
- w_query: bfloat16 [2048, 2048], P('dp', 'mp'), may hold values from -0.125 to 0.125
- w_key: bfloat16 [2048, 256], P('dp', 'mp'), may hold values from -0.125 to 0.125
- w_value: bfloat16 [2048, 256], P('dp', 'mp'), may hold values from -0.125 to 0.125
- w_out: bfloat16 [2048, 2048], P('mp', 'dp'), may hold values from -0.375 to 0.375
- w_gate: bfloat16 [2048, 5632], P('dp', 'mp'), may hold values from -0.125 to 0.125
- w_up: bfloat16 [2048, 5632], P('dp', 'mp'), may hold values from -0.125 to 0.125
- w_down: bfloat16 [5632, 2048], P('mp', 'dp'), may hold values from -0.078125 to 0.078125
- attn_gain: bfloat16 [2048], P('dp'), may hold values from 0.25 to 1.75
- mlp_gain: bfloat16 [2048], P('dp'), may hold values from 0.25 to 1.75
- cotangent: bfloat16 [8192, 2048], P('dp'), may hold values from -6 to 6
Outputs:
- output: bfloat16 [8192, 2048], P('dp')
- input_grad: float32 [8192, 2048], P('dp')
- grad_w_query: float32 [2048, 2048], P('dp', 'mp')
- grad_w_key: float32 [2048, 256], P('dp', 'mp')
- grad_w_value: float32 [2048, 256], P('dp', 'mp')
- grad_w_out: float32 [2048, 2048], P('mp', 'dp')
- grad_w_gate: float32 [2048, 5632], P('dp', 'mp')
- grad_w_up: float32 [2048, 5632], P('dp', 'mp')
- grad_w_down: float32 [5632, 2048], P('mp', 'dp')
- grad_attn_gain: float32 [2048], P('dp')
- grad_mlp_gain: float32 [2048], P('dp')
Inputs may be any that keep to these rules, and one draw needn't show every extreme that they name: `doc_ids`: within a sequence the ids never fall; a document spans 1 to 256 tokens and one spans exactly 256.
All inputs are finite; a program needn't handle non-finite values. No bound on the sum of `selection` on one device may be relied on, other than what follows from the above.
Results may differ from a plain program's by a relative error of at most 0.024.
Values may be sent and summed in bfloat16 or wider, within the bound.
A program may use at most 256 MiB of HBM per device.

v0:
```python
import jax
import jax.numpy as jnp
from jax import lax
from jax.sharding import PartitionSpec as P

HEAD_DIM = 64
EPSILON = 1e-05
MASKED = -1e30


def rope_tables(length, head_width):
    half_width = head_width // 2
    frequency = 10000.0 ** (-2.0 * jnp.arange(half_width, dtype=jnp.float32) / head_width)
    places = jnp.arange(length, dtype=jnp.float32)
    angles = places[:, None] * frequency[None, :]
    return (jnp.cos(angles)[:, None, :], jnp.sin(angles)[:, None, :])


def rotate(field, cosine_table, sine_table):
    half_width = field.shape[-1] // 2
    first_half = field[..., :half_width]
    second_half = field[..., half_width:]
    return jnp.concatenate(
        [
            first_half * cosine_table - second_half * sine_table,
            second_half * cosine_table + first_half * sine_table,
        ],
        axis=-1,
    )


def allowed_pairs(doc_row):
    length = doc_row.shape[0]
    query_index = lax.broadcasted_iota(jnp.int32, (length, length), 0)
    key_index = lax.broadcasted_iota(jnp.int32, (length, length), 1)
    return (doc_row[:, None] == doc_row[None, :]) & (query_index >= key_index)


def rms_forward(residual, gain_row):
    inverse = lax.rsqrt(jnp.mean(residual * residual, axis=-1, keepdims=True) + EPSILON)
    return (residual * inverse * gain_row, inverse)


def rms_backward(residual, inverse, gain_row, grad_normed):
    scaled = grad_normed * gain_row
    gain_part = jnp.sum(grad_normed * residual * inverse, axis=0)
    mean_term = jnp.mean(scaled * residual, axis=-1, keepdims=True)
    return (inverse * scaled - residual * (inverse * inverse * inverse) * mean_term, gain_part)


def attend_forward(queries, key_rows, value_rows, doc_row, score_scale):
    length, kv_local, head_width = key_rows.shape
    grouped = queries.reshape(length, kv_local, -1, head_width)
    scores = (
        jnp.einsum("qkgd,skd->kgqs", grouped, key_rows, preferred_element_type=jnp.float32)
        * score_scale
    )
    scores = jnp.where(allowed_pairs(doc_row), scores, MASKED)
    highest = jnp.max(scores, axis=-1, keepdims=True)
    shifted_exp = jnp.exp(scores - highest)
    totals = jnp.sum(shifted_exp, axis=-1, keepdims=True)
    probs_low = (shifted_exp / totals).astype(jnp.bfloat16)
    mixed_heads = jnp.einsum(
        "kgqs,skd->qkgd", probs_low, value_rows, preferred_element_type=jnp.float32
    )
    return (mixed_heads.reshape(length, -1), highest + jnp.log(totals))


def attend_backward(queries, key_rows, value_rows, doc_row, logsum, grad_mixed, score_scale):
    length, kv_local, head_width = key_rows.shape
    grouped = queries.reshape(length, kv_local, -1, head_width)
    grad_grouped = grad_mixed.reshape(length, kv_local, -1, head_width)
    scores = (
        jnp.einsum("qkgd,skd->kgqs", grouped, key_rows, preferred_element_type=jnp.float32)
        * score_scale
    )
    attn_probs = jnp.where(allowed_pairs(doc_row), jnp.exp(scores - logsum), 0.0)
    grad_probs = jnp.einsum(
        "qkgd,skd->kgqs", grad_grouped, value_rows, preferred_element_type=jnp.float32
    )
    inner_sum = jnp.sum(attn_probs * grad_probs, axis=-1, keepdims=True)
    grad_scores = (attn_probs * (grad_probs - inner_sum)).astype(jnp.bfloat16)
    grad_queries = (
        jnp.einsum("kgqs,skd->qkgd", grad_scores, key_rows, preferred_element_type=jnp.float32)
        * score_scale
    )
    grad_keys = (
        jnp.einsum("kgqs,qkgd->skd", grad_scores, grouped, preferred_element_type=jnp.float32)
        * score_scale
    )
    grad_values = jnp.einsum(
        "kgqs,qkgd->skd",
        attn_probs.astype(jnp.bfloat16),
        grad_grouped,
        preferred_element_type=jnp.float32,
    )
    return (grad_queries.reshape(length, -1, head_width), grad_keys, grad_values)


def per_device(
    tokens,
    doc_ids,
    selection,
    w_query,
    w_key,
    w_value,
    w_out,
    w_gate,
    w_up,
    w_down,
    attn_gain,
    mlp_gain,
    cotangent,
):
    (
        full_query,
        full_key,
        full_value,
        full_out,
        full_gate,
        full_up,
        full_down,
        gathered_one,
        gathered_two,
    ) = (
        lax.all_gather(w_query, "dp", axis=0, tiled=True),
        lax.all_gather(w_key, "dp", axis=0, tiled=True),
        lax.all_gather(w_value, "dp", axis=0, tiled=True),
        lax.all_gather(w_out, "dp", axis=1, tiled=True),
        lax.all_gather(w_gate, "dp", axis=0, tiled=True),
        lax.all_gather(w_up, "dp", axis=0, tiled=True),
        lax.all_gather(w_down, "dp", axis=1, tiled=True),
        lax.all_gather(attn_gain, "dp", axis=0, tiled=True),
        lax.all_gather(mlp_gain, "dp", axis=0, tiled=True),
    )
    gain_one = gathered_one.astype(jnp.float32)
    gain_two = gathered_two.astype(jnp.float32)
    seq_local, length = doc_ids.shape
    tok_local = seq_local * length
    heads_local = full_query.shape[1] // HEAD_DIM
    kv_local = full_key.shape[1] // HEAD_DIM
    score_scale = HEAD_DIM ** (-0.5)
    cosine_table, sine_table = rope_tables(length, HEAD_DIM)
    residual = tokens.astype(jnp.float32)
    normed_float, inverse_one = rms_forward(residual, gain_one)
    normed_one = normed_float.astype(jnp.bfloat16)
    query_lin = jnp.dot(normed_one, full_query, preferred_element_type=jnp.float32).reshape(
        seq_local, length, heads_local, HEAD_DIM
    )
    key_lin = jnp.dot(normed_one, full_key, preferred_element_type=jnp.float32).reshape(
        seq_local, length, kv_local, HEAD_DIM
    )
    value_rows = (
        jnp.dot(normed_one, full_value, preferred_element_type=jnp.float32)
        .astype(jnp.bfloat16)
        .reshape(seq_local, length, kv_local, HEAD_DIM)
    )
    query_rot = rotate(query_lin, cosine_table, sine_table).astype(jnp.bfloat16)
    key_rot = rotate(key_lin, cosine_table, sine_table).astype(jnp.bfloat16)

    def forward_one(bundle):
        return attend_forward(bundle[0], bundle[1], bundle[2], bundle[3], score_scale)

    mixed_heads, logsum = lax.map(forward_one, (query_rot, key_rot, value_rows, doc_ids))
    mixed_low = mixed_heads.reshape(tok_local, heads_local * HEAD_DIM).astype(jnp.bfloat16)
    attn_partial = jnp.dot(mixed_low, full_out, preferred_element_type=jnp.float32)
    hidden_in = residual + lax.psum(attn_partial.astype(jnp.bfloat16), "mp").astype(jnp.float32)
    normed_two_float, inverse_two = rms_forward(hidden_in, gain_two)
    normed_two = normed_two_float.astype(jnp.bfloat16)
    gate_lin = jnp.dot(normed_two, full_gate, preferred_element_type=jnp.float32)
    up_lin = jnp.dot(normed_two, full_up, preferred_element_type=jnp.float32)
    sig_gate = jax.nn.sigmoid(gate_lin)
    swish_gate = gate_lin * sig_gate
    hidden = (swish_gate * up_lin).astype(jnp.bfloat16)
    mlp_partial = jnp.dot(hidden, full_down, preferred_element_type=jnp.float32)
    output = (
        hidden_in + lax.psum(mlp_partial.astype(jnp.bfloat16), "mp").astype(jnp.float32)
    ).astype(jnp.bfloat16)
    grad_y = cotangent.astype(jnp.float32) * selection.reshape(tok_local, 1).astype(jnp.float32)
    grad_y_low = grad_y.astype(jnp.bfloat16)
    grad_down = jnp.einsum("tf,td->fd", hidden, grad_y_low, preferred_element_type=jnp.float32)
    grad_hidden = jnp.einsum("td,fd->tf", grad_y_low, full_down, preferred_element_type=jnp.float32)
    grad_gate_low = (grad_hidden * up_lin * sig_gate * (1.0 + gate_lin * (1.0 - sig_gate))).astype(
        jnp.bfloat16
    )
    grad_up_low = (grad_hidden * swish_gate).astype(jnp.bfloat16)
    grad_gate_w = jnp.einsum(
        "td,tf->df", normed_two, grad_gate_low, preferred_element_type=jnp.float32
    )
    grad_up_w = jnp.einsum("td,tf->df", normed_two, grad_up_low, preferred_element_type=jnp.float32)
    partial_two = jnp.einsum(
        "tf,df->td", grad_gate_low, full_gate, preferred_element_type=jnp.float32
    ) + jnp.einsum("tf,df->td", grad_up_low, full_up, preferred_element_type=jnp.float32)
    grad_normed_two = lax.psum(partial_two.astype(jnp.bfloat16), "mp").astype(jnp.float32)
    grad_resid_two, gain_grad_two = rms_backward(hidden_in, inverse_two, gain_two, grad_normed_two)
    grad_h = grad_y + grad_resid_two
    grad_h_low = grad_h.astype(jnp.bfloat16)
    grad_out_w = jnp.einsum("tc,td->cd", mixed_low, grad_h_low, preferred_element_type=jnp.float32)
    grad_mixed = jnp.einsum(
        "td,cd->tc", grad_h_low, full_out, preferred_element_type=jnp.float32
    ).astype(jnp.bfloat16)
    grad_mixed = grad_mixed.reshape(seq_local, length, heads_local * HEAD_DIM)

    def backward_one(bundle):
        return attend_backward(
            bundle[0], bundle[1], bundle[2], bundle[3], bundle[4], bundle[5], score_scale
        )

    grad_query_rot, grad_key_rot, grad_values = lax.map(
        backward_one, (query_rot, key_rot, value_rows, doc_ids, logsum, grad_mixed)
    )
    grad_query_lin = (
        rotate(grad_query_rot, cosine_table, -sine_table)
        .reshape(tok_local, heads_local * HEAD_DIM)
        .astype(jnp.bfloat16)
    )
    grad_key_lin = (
        rotate(grad_key_rot, cosine_table, -sine_table)
        .reshape(tok_local, kv_local * HEAD_DIM)
        .astype(jnp.bfloat16)
    )
    grad_value_low = grad_values.reshape(tok_local, kv_local * HEAD_DIM).astype(jnp.bfloat16)
    grad_query_w = jnp.einsum(
        "td,tc->dc", normed_one, grad_query_lin, preferred_element_type=jnp.float32
    )
    grad_key_w = jnp.einsum(
        "td,tc->dc", normed_one, grad_key_lin, preferred_element_type=jnp.float32
    )
    grad_value_w = jnp.einsum(
        "td,tc->dc", normed_one, grad_value_low, preferred_element_type=jnp.float32
    )
    partial_one = (
        jnp.einsum("tc,dc->td", grad_query_lin, full_query, preferred_element_type=jnp.float32)
        + jnp.einsum("tc,dc->td", grad_key_lin, full_key, preferred_element_type=jnp.float32)
        + jnp.einsum("tc,dc->td", grad_value_low, full_value, preferred_element_type=jnp.float32)
    )
    grad_normed_one = lax.psum(partial_one.astype(jnp.bfloat16), "mp").astype(jnp.float32)
    grad_resid_one, gain_grad_one = rms_backward(residual, inverse_one, gain_one, grad_normed_one)
    input_grad = grad_h + grad_resid_one
    (
        shard_query,
        shard_key,
        shard_value,
        shard_out,
        shard_gate,
        shard_up,
        shard_down,
        shard_gain_one,
        shard_gain_two,
    ) = (
        lax.psum_scatter(
            grad_query_w.astype(jnp.bfloat16), "dp", scatter_dimension=0, tiled=True
        ).astype(jnp.float32),
        lax.psum_scatter(
            grad_key_w.astype(jnp.bfloat16), "dp", scatter_dimension=0, tiled=True
        ).astype(jnp.float32),
        lax.psum_scatter(
            grad_value_w.astype(jnp.bfloat16), "dp", scatter_dimension=0, tiled=True
        ).astype(jnp.float32),
        lax.psum_scatter(
            grad_out_w.astype(jnp.bfloat16), "dp", scatter_dimension=1, tiled=True
        ).astype(jnp.float32),
        lax.psum_scatter(
            grad_gate_w.astype(jnp.bfloat16), "dp", scatter_dimension=0, tiled=True
        ).astype(jnp.float32),
        lax.psum_scatter(
            grad_up_w.astype(jnp.bfloat16), "dp", scatter_dimension=0, tiled=True
        ).astype(jnp.float32),
        lax.psum_scatter(
            grad_down.astype(jnp.bfloat16), "dp", scatter_dimension=1, tiled=True
        ).astype(jnp.float32),
        lax.psum_scatter(
            gain_grad_one.astype(jnp.bfloat16), "dp", scatter_dimension=0, tiled=True
        ).astype(jnp.float32),
        lax.psum_scatter(
            gain_grad_two.astype(jnp.bfloat16), "dp", scatter_dimension=0, tiled=True
        ).astype(jnp.float32),
    )
    return (
        output,
        input_grad,
        shard_query,
        shard_key,
        shard_value,
        shard_out,
        shard_gate,
        shard_up,
        shard_down,
        shard_gain_one,
        shard_gain_two,
    )


def solution(mesh):
    in_specs = (
        P("dp", None),
        P("dp", None),
        P("dp", None),
        P("dp", "mp"),
        P("dp", "mp"),
        P("dp", "mp"),
        P("mp", "dp"),
        P("dp", "mp"),
        P("dp", "mp"),
        P("mp", "dp"),
        P("dp"),
        P("dp"),
        P("dp", None),
    )
    out_specs = (
        P("dp", None),
        P("dp", None),
        P("dp", "mp"),
        P("dp", "mp"),
        P("dp", "mp"),
        P("mp", "dp"),
        P("dp", "mp"),
        P("dp", "mp"),
        P("mp", "dp"),
        P("dp"),
        P("dp"),
    )
    return jax.shard_map(
        per_device, mesh=mesh, in_specs=in_specs, out_specs=out_specs, check_vma=False
    )
```

profile of v0, /device:TPU:0, one launch (start us, length us, event | category | flops | bytes accessed | tf_op | source)
XLA Modules:
  0.0 1349.3 jit_solution(685220449423602048)
XLA Ops:
  13.4 10.4 all-gather
  24.8 10.8 all_gather.29
  35.6 9.4 all_gather.28
  68.6 15.0 %while.26 = (s32[]{:T(128)}, bf16[2,512,512]{2,1,0:T(8,128)(2,1)S(1)}, f32[2,1,8,512,1]{3,2,4,1,0:T(8,128)}, bf16[2,512,1,64]{1,3,2,0:T(8,128)(2,1)S(1)}, s32[2,...) while((s32[]{:T(128)}, ...), condition=%wide.region_4.5_spmd, body=%wide.region_1.4_spmd.sunk | while | flops 562819072 | bytes 29629548 | solution.py:164
  91.9 8.8 all-gather.1
  100.7 144.7 %all-reduce.8.cloned.1.call-done = bf16[1024,2048]{1,0:T(8,128)(2,1)} async-done(((bf16[1024,2048]{1,0:T(8,128)(2,1)}), bf16[1024,2048]{1,0:T(8,128)(2,1)}) %all-reduce.8.cloned.1.call-update) | async-done | bytes 4194320 | tf_op jit(solution)/shard_map/psum | solution.py:167
  255.4 34.0 %all-gather.14.cloned.1.call-done = bf16[2048,1408]{1,0:T(8,128)(2,1)} async-done(((bf16[256,1408]{1,0:T(8,128)(2,1)}), bf16[2048,1408]{1,0:T(8,128)(2,1)}) %all-gather.14.cloned.1.call-update) | async-done | bytes 5767184 | tf_op jit(solution)/shard_map/all_gather | solution.py:131
  289.3 11.7 fusion.91
  301.0 33.3 %all-gather.12.cloned.1.call-done = bf16[2048,1408]{1,0:T(8,128)(2,1)} async-done(((bf16[256,1408]{1,0:T(8,128)(2,1)}), bf16[2048,1408]{1,0:T(8,128)(2,1)}) %all-gather.12.cloned.1.call-update) | async-done | bytes 5767184 | tf_op jit(solution)/shard_map/all_gather | solution.py:130
  334.3 11.7 fusion.90
  346.0 34.3 %all-gather.16.cloned.1.call-done = bf16[1408,2048]{1,0:T(8,128)(2,1)} async-done(((bf16[1408,256]{1,0:T(8,128)(2,1)}), bf16[1408,2048]{1,0:T(8,128)(2,1)}) %all-gather.16.cloned.1.call-update) | async-done | bytes 5767184 | tf_op jit(solution)/shard_map/all_gather | solution.py:132
  380.3 17.0 %multiply_convert_fusion.1 = (bf16[1024,1408]{1,0:T(8,128)(2,1)}, bf16[1024,1408]{1,0:T(8,128)(2,1)}, bf16[1024,1408]{1,0:T(8,128)(2,1)}) fusion(f32[1024,1408]{1,0:T(8,128)} %fusion.90, f32[1024,1408]{1,0:T(8,128)} %fusion.91, bf16[1408,2048]{1,0:T(8,128)(2,1)} %all-gather.16.cloned.1.call-done, bf16[1024,2048]{1,0:T(8,128)(2,1)} %param.29, ...), kind=kOutput, calls=%fused_computation.103 | convolution fusion | flops 5933498368 | bytes 30150656 | tf_op jit(solution)/shard_map/td,fd->tf/dot_general | solution.py:182
  397.3 8.7 fusion.92
  406.0 11.0 add_convert_fusion.1
  417.1 155.1 %all-reduce.10.cloned.1.call-done = bf16[1024,2048]{1,0:T(8,128)(2,1)} async-done(((bf16[1024,2048]{1,0:T(8,128)(2,1)}), bf16[1024,2048]{1,0:T(8,128)(2,1)}) %all-reduce.10.cloned.1.call-update) | async-done | bytes 4194320 | tf_op jit(solution)/shard_map/psum | solution.py:194
  572.1 8.6 fusion.65
  590.2 70.1 %while.27 = (s32[]{:T(128)}, f32[2,512,8,64]{1,0,3,2:T(2,128)}, f32[2,512,1,64]{1,3,2,0:T(8,128)}, bf16[2,512,1,64]{1,3,2,0:T(8,128)(2,1)}, bf16[2,512,1,64]{1,3...) while((s32[]{:T(128)}, f32[2,512,8,64]{1,0,3,2:T(2,128)}, ...), condition=%wide.region_12.13_spmd, body=%wide.region_10.12_spmd.sunk | while | flops 1374711808 | bytes 77127944 | solution.py:209
  605.9 19.6 %dynamic_update_slice.32 = f32[2,512,8,64]{1,0,3,2:T(2,128)} dynamic-update-slice(f32[2,512,8,64]{1,0,3,2:T(2,128)} %get-tuple-element.378, f32[1,512,8,64]{1,0,3,2:T(1,128)S(1)} %copy.100, s32[]{:T(128)S(6)} %copy.121, s32[]{:T(128)} %constant.66.clone.1..sunk, s32[]{:T(128)} %constant.66.clone.1..sunk, s32[]{:T(128)} %constant.66.clone.1..sunk) | dynamic-update-slice | bytes 2097156 | tf_op jit(solution)/shard_map/while/body/jit(dynamic_update_index_in_dim)/dynamic_update_slice | solution.py:209
  640.7 19.6 %dynamic_update_slice.32 = f32[2,512,8,64]{1,0,3,2:T(2,128)} dynamic-update-slice(f32[2,512,8,64]{1,0,3,2:T(2,128)} %get-tuple-element.378, f32[1,512,8,64]{1,0,3,2:T(1,128)S(1)} %copy.100, s32[]{:T(128)S(6)} %copy.121, s32[]{:T(128)} %constant.66.clone.1..sunk, s32[]{:T(128)} %constant.66.clone.1..sunk, s32[]{:T(128)} %constant.66.clone.1..sunk) | dynamic-update-slice | bytes 2097156 | tf_op jit(solution)/shard_map/while/body/jit(dynamic_update_index_in_dim)/dynamic_update_slice | solution.py:209
  680.9 7.1 convolution_convert_fusion.5
  688.0 11.0 convolution_convert_fusion.1
  699.1 11.0 convolution_convert_fusion.2
  710.7 10.9 convolution_convert_fusion
  721.9 10.9 convolution_convert_fusion.3
  744.7 37.6 %reduce-scatter.8.cloned.1.call-done = bf16[256,512]{1,0:T(8,128)(2,1)} async-done(((bf16[2048,512]{1,0:T(8,128)(2,1)}), bf16[256,512]{1,0:T(8,128)(2,1)}) %reduce-scatter.8.cloned.1.call-update) | async-done | bytes 262160 | tf_op jit(solution)/shard_map/reduce_scatter | solution.py:251
  784.1 42.6 %reduce-scatter.14.cloned.1.call-done = bf16[512,256]{1,0:T(8,128)(2,1)} async-done(((bf16[512,2048]{1,0:T(8,128)(2,1)}), bf16[512,256]{1,0:T(8,128)(2,1)}) %reduce-scatter.14.cloned.1.call-update) | async-done | bytes 262160 | tf_op jit(solution)/shard_map/reduce_scatter | solution.py:260
  828.6 60.6 %reduce-scatter.18.cloned.1.call-done = bf16[256,1408]{1,0:T(8,128)(2,1)} async-done(((bf16[2048,1408]{1,0:T(8,128)(2,1)}), bf16[256,1408]{1,0:T(8,128)(2,1)}) %reduce-scatter.18.cloned.1.call-update) | async-done | bytes 720912 | tf_op jit(solution)/shard_map/reduce_scatter | solution.py:266
  891.4 60.2 %reduce-scatter.16.cloned.1.call-done = bf16[256,1408]{1,0:T(8,128)(2,1)} async-done(((bf16[2048,1408]{1,0:T(8,128)(2,1)}), bf16[256,1408]{1,0:T(8,128)(2,1)}) %reduce-scatter.16.cloned.1.call-update) | async-done | bytes 720912 | tf_op jit(solution)/shard_map/reduce_scatter | solution.py:263
  954.0 59.9 %reduce-scatter.20.cloned.1.call-done = bf16[1408,256]{1,0:T(8,128)(2,1)} async-done(((bf16[1408,2048]{1,0:T(8,128)(2,1)}), bf16[1408,256]{1,0:T(8,128)(2,1)}) %reduce-scatter.20.cloned.1.call-update) | async-done | bytes 720912 | tf_op jit(solution)/shard_map/reduce_scatter | solution.py:269
  1016.2 291.6 %all-reduce.12.cloned.1.call-done = (bf16[1024,2048]{1,0:T(8,128)(2,1)}, bf16[1024,2048]{1,0:T(8,128)(2,1)}) async-done(((bf16[1024,2048]{1,0:T(8,128)(2,1)}, bf16[1024,2048]{1,0:T(8,128)(2,1)}), (bf16[1024,2048]{1,0:T(8,128)(2,1)}, bf16[1024,2048]{1,0:T(8,128)(2,1)})) %all-reduce.12.cloned.1.call-update) | async-done | bytes 8388624 | tf_op jit(solution)/shard_map/psum | solution.py:177
  1313.4 13.7 %all-reduce.2 = (bf16[2048]{0:T(1024)(128)(2,1)S(1)}, bf16[2048]{0:T(1024)(128)(2,1)S(1)}) all-reduce(bf16[2048]{0:T(1024)(128)(2,1)S(1)} %get-tuple-element.161, bf16[2048]{0:T(1024)(128)(2,1)S(1)} %copy-done.24), channel_id=9, replica_groups=mesh['dp'=8,'mp'=4] {'dp'}, use_global_device_ids=true, to_apply=%region_23.24.clone | all-reduce | flops 4096 | bytes 16384
  1327.8 14.6 %fusion.60 = (f32[1024,2048]{1,0:T(8,128)}, bf16[1024,2048]{1,0:T(8,128)(2,1)}) fusion(f32[1024,2048]{1,0:T(8,128)} %copy-done.6, bf16[1024,2048]{1,0:T(8,128)(2,1)} %get-tuple-element.200, bf16[1024,2048]{1,0:T(8,128)(2,1)} %param.17, f32[1024]{0:T(1024)S(1)} %broadcast_multiply_fusion, f32[1024]{0:T(1024)S(1)} %copy-done.23, f32[2048]{0:T(1024)S(1)} %bitcast.299, ...), kind=kLoop, calls=%fused_computation.80 | loop fusion | flops 27262976 | bytes 37769216 | tf_op jit(solution)/shard_map/add | solution.py:239
  (212 shorter events, 153.0 us)
Async XLA Ops:
  7.2 46.4 %all-gather.8.cloned.1.call-start = ((), (), s32[]{:S(2)}) async-start(), calls=%async_computation.7 | async-start | bytes 2359296 | tf_op jit(solution)/shard_map/all_gather | solution.py:126
  7.9 75.8 %all-gather.10.cloned.1.call-start = ((), (), s32[]{:S(2)}) async-start(), calls=%async_computation.8 | async-start | bytes 2359296 | tf_op jit(solution)/shard_map/all_gather | solution.py:129
  8.7 236.7 %all-reduce.8.cloned.1.call-start = ((), (), s32[]{:S(2)}) async-start(), calls=%async_computation.9 | async-start | bytes 8388608 | tf_op jit(solution)/shard_map/psum | solution.py:167
  8.7 36.2 %copy-start = (bf16[1024,2048]{1,0:T(8,128)(2,1)S(1)}, bf16[1024,2048]{1,0:T(8,128)(2,1)}, u32[]{:S(2)}) copy-start(bf16[1024,2048]{1,0:T(8,128)(2,1)} %param.17) | copy-start | bytes 12582916
  13.4 32.6 %copy-start.21 = (f32[1024]{0:T(1024)}, f32[1024]{0:T(1024)S(1)}, u32[]{:S(2)}) copy-start(f32[1024]{0:T(1024)S(1)} %get-tuple-element.221) | copy-start | bytes 12292
  23.8 22.1 %copy-start.19 = (f32[8,1,256]{2,1,0:T(1,128)}, f32[8,1,256]{2,1,0:T(1,128)S(1)}, u32[]{:S(2)}) copy-start(f32[8,1,256]{2,1,0:T(1,128)S(1)} %convert_element_type.218) | copy-start | bytes 24580
  24.8 39.6 %copy-start.12 = (f32[512,32]{0,1:T(8,128)}, f32[512,32]{0,1:T(8,128)S(1)}, u32[]{:S(2)}) copy-start(f32[512,32]{0,1:T(8,128)S(1)} %get-tuple-element.226) | copy-start | bytes 196612
  35.6 13.9 %copy-start.8 = (bf16[2048,64]{0,1:T(8,128)(2,1)}, bf16[2048,64]{0,1:T(8,128)(2,1)S(1)}, u32[]{:S(2)}) copy-start(bf16[2048,64]{0,1:T(8,128)(2,1)S(1)} %all_gather.29) | copy-start | bytes 786436
  83.7 6.3 copy-start.15
  90.1 199.3 %all-gather.14.cloned.1.call-start = ((), (), s32[]{:S(2)}) async-start(), calls=%async_computation.11 | async-start | bytes 6488064 | tf_op jit(solution)/shard_map/all_gather | solution.py:131
  90.6 243.6 %all-gather.12.cloned.1.call-start = ((), (), s32[]{:S(2)}) async-start(), calls=%async_computation.10 | async-start | bytes 6488064 | tf_op jit(solution)/shard_map/all_gather | solution.py:130
  91.2 289.1 %all-gather.16.cloned.1.call-start = ((), (), s32[]{:S(2)}) async-start(), calls=%async_computation.12 | async-start | bytes 6488064 | tf_op jit(solution)/shard_map/all_gather | solution.py:132
  91.8 480.3 %all-reduce.10.cloned.1.call-start = ((), (), s32[]{:S(2)}) async-start(), calls=%async_computation.13 | async-start | bytes 8388608 | tf_op jit(solution)/shard_map/psum | solution.py:194
  91.9 488.8 %copy-start.25 = (f32[1,4,2,128]{3,1,2,0:T(4,128)}, f32[1,4,2,128]{3,1,2,0:T(4,128)S(1)}, u32[]{:S(2)}) copy-start(f32[1,4,2,128]{3,1,2,0:T(4,128)S(1)} %copy.87) | copy-start | bytes 12292
  380.3 17.0 %copy-start.28 = (bf16[2048,1408]{1,0:T(8,128)(2,1)S(1)}, bf16[2048,1408]{1,0:T(8,128)(2,1)}, u32[]{:S(2)}) copy-start(bf16[2048,1408]{1,0:T(8,128)(2,1)} %all-gather.12.cloned.1.call-done) | copy-start | bytes 17301508
  397.3 8.7 copy-start.33
  417.0 324.9 %reduce-scatter.10.cloned.1.call-start = ((), (), s32[]{:S(2)}) async-start(), calls=%async_computation.15 | async-start | bytes 294912 | tf_op jit(solution)/shard_map/reduce_scatter | solution.py:254
  572.1 8.6 copy-start.2
  572.1 8.6 copy-start.5
  572.1 8.6 copy-start.7
  668.0 75.3 %reduce-scatter.12.cloned.1.call-start = ((), (), s32[]{:S(2)}) async-start(), calls=%async_computation.16 | async-start | bytes 294912 | tf_op jit(solution)/shard_map/reduce_scatter | solution.py:257
  674.7 107.7 %reduce-scatter.8.cloned.1.call-start = ((), (), s32[]{:S(2)}) async-start(), calls=%async_computation.14 | async-start | bytes 2359296 | tf_op jit(solution)/shard_map/reduce_scatter | solution.py:251
  680.8 146.0 %reduce-scatter.14.cloned.1.call-start = ((), (), s32[]{:S(2)}) async-start(), calls=%async_computation.17 | async-start | bytes 2359296 | tf_op jit(solution)/shard_map/reduce_scatter | solution.py:260
  687.9 201.2 %reduce-scatter.18.cloned.1.call-start = ((), (), s32[]{:S(2)}) async-start(), calls=%async_computation.19 | async-start | bytes 6488064 | tf_op jit(solution)/shard_map/reduce_scatter | solution.py:266
  699.0 252.6 %reduce-scatter.16.cloned.1.call-start = ((), (), s32[]{:S(2)}) async-start(), calls=%async_computation.18 | async-start | bytes 6488064 | tf_op jit(solution)/shard_map/reduce_scatter | solution.py:263
  710.1 303.8 %reduce-scatter.20.cloned.1.call-start = ((), (), s32[]{:S(2)}) async-start(), calls=%async_computation.20 | async-start | bytes 6488064 | tf_op jit(solution)/shard_map/reduce_scatter | solution.py:269
  721.6 11.2 copy-start.9
  721.6 586.1 %all-reduce.12.cloned.1.call-start = ((), (), s32[]{:S(2)}) async-start(), calls=%async_computation.21 | async-start | bytes 16777216 | tf_op jit(solution)/shard_map/psum | solution.py:177
  740.0 567.7 %copy-start.20 = (f32[8,1,256]{2,1,0:T(1,128)S(1)}, f32[8,1,256]{2,1,0:T(1,128)}, u32[]{:S(2)}) copy-start(f32[8,1,256]{2,1,0:T(1,128)} %copy-done.19) | copy-start | bytes 24580
  740.0 567.7 %copy-start.22 = (f32[1024]{0:T(1024)S(1)}, f32[1024]{0:T(1024)}, u32[]{:S(2)}) copy-start(f32[1024]{0:T(1024)} %copy-done.21) | copy-start | bytes 12292
  953.9 359.5 %copy-start.24 = (bf16[2048]{0:T(1024)(128)(2,1)S(1)}, bf16[2048]{0:T(1024)(128)(2,1)}, u32[]{:S(2)}) copy-start(bf16[2048]{0:T(1024)(128)(2,1)} %get-tuple-element.159) | copy-start | bytes 12292
  953.9 373.8 %copy-start.23 = (f32[1024]{0:T(1024)S(1)}, f32[1024]{0:T(1024)}, u32[]{:S(2)}) copy-start(f32[1024]{0:T(1024)} %get-tuple-element.220) | copy-start | bytes 12292
  (21 other events, 56.7 us)
Sparse Core Ops, SparseCore 0:
  9.9 30.9 all-gather.7
  42.7 28.2 all-gather.9
  90.2 155.1 all-reduce.7
  247.1 42.1 all-gather.13
  291.0 43.1 all-gather.11
  336.0 44.2 all-gather.15
  417.1 154.9 all-reduce.9
  668.1 32.6 reduce-scatter.9
  704.4 33.6 reduce-scatter.11
  741.2 41.0 reduce-scatter.7
  785.6 41.1 reduce-scatter.13
  830.1 59.0 reduce-scatter.17
  892.6 59.0 reduce-scatter.15
  954.9 58.8 reduce-scatter.19
  1016.9 290.8 all-reduce.11
where the time goes:
time: 1360 us; the launch traced here: 1350 us
  waiting for transfers between devices  957 us (70%)
  matrix products  177 us (13%)
  other arithmetic  83.6 us (6%)
  local copies, waits for them, and re-layouts  61.2 us (4%)
  blocking collectives  53 us (4%)
  between operations  15.5 us (1%)
    psum x1, waiting for transfers between devices, per_device(): lax.psum(mlp_partial.astype(jnp.bfloat16), 'mp').astype(jnp.float32)  292 us
    psum x1, waiting for transfers between devices, per_device(): lax.psum(partial_two.astype(jnp.bfloat16), 'mp').astype(jnp.float32)  155 us
    psum x1, waiting for transfers between devices, per_device(): lax.psum(attn_partial.astype(jnp.bfloat16), 'mp').astype(jnp.float32)  145 us
    reduce_scatter x1, waiting for transfers between devices, per_device(): lax.psum_scatter(grad_up_w.astype(jnp.bfloat16), 'dp', scatter_dimension=...  60.6 us
    reduce_scatter x1, waiting for transfers between devices, per_device(): lax.psum_scatter(grad_gate_w.astype(jnp.bfloat16), 'dp', scatter_dimensio...  60.2 us
    reduce_scatter x1, waiting for transfers between devices, per_device(): lax.psum_scatter(grad_down.astype(jnp.bfloat16), 'dp', scatter_dimension=...  59.9 us
    reduce_scatter x1, waiting for transfers between devices, per_device(): lax.psum_scatter(grad_out_w.astype(jnp.bfloat16), 'dp', scatter_dimension...  42.6 us
    dynamic_update_slice x4, local copies, waits for them, and re-layouts, per_device(): lax.map(backward_one, (query_rot, key_rot, value_rows, doc_ids, logsum, g...  41.4 us
  transfers between devices with their start and end apart: 15, of which 11 were waited for; matrix products, arithmetic and copies ran while one was open for 12% of the time, Pallas kernels for 0%

commit v1 on v0

--- a/solution.py
+++ b/solution.py
@@ -2,6 +2,7 @@
 import jax.numpy as jnp
 from jax import lax
 from jax.sharding import PartitionSpec as P
+from jax.lax import all_gather
 
 HEAD_DIM = 64
 EPSILON = 1e-05
@@ -174,7 +175,8 @@
     hidden = (swish_gate * up_lin).astype(jnp.bfloat16)
     mlp_partial = jnp.dot(hidden, full_down, preferred_element_type=jnp.float32)
     output = (
-        hidden_in + lax.psum(mlp_partial.astype(jnp.bfloat16), "mp").astype(jnp.float32)
+        hidden_in
+        + jnp.sum(all_gather(mlp_partial.astype(jnp.bfloat16), "mp"), 0).astype(jnp.float32)
     ).astype(jnp.bfloat16)
     grad_y = cotangent.astype(jnp.float32) * selection.reshape(tok_local, 1).astype(jnp.float32)
     grad_y_low = grad_y.astype(jnp.bfloat16)

time: 1360 us -> 1410 us (1.037)
  matrix products: 177 us -> 200 us
  waiting for transfers between devices: 957 us -> 972 us
    all_gather x0 -> x1, waiting for transfers between devices: none -> 280 us  [per_device(): all_gather(mlp_partial.astype(jnp.bfloat16), 'mp')]
    psum x1, waiting for transfers between devices: 292 us -> 155 us  [per_device(): lax.psum(partial_one.astype(jnp.bfloat16), 'mp').astype(jnp.float32)]
    reduce_scatter x1, waiting for transfers between devices: 60.6 us -> 0.01 us  [per_device(): lax.psum_scatter(grad_up_w.astype(jnp.bfloat16), 'dp', scatter_dimension=...]
    reduce_scatter x1, waiting for transfers between devices: 60.2 us -> 0.02 us  [per_device(): lax.psum_scatter(grad_gate_w.astype(jnp.bfloat16), 'dp', scatter_dimensio...]
    psum x1, waiting for transfers between devices: 155 us -> 110 us  [per_device(): lax.psum(partial_two.astype(jnp.bfloat16), 'mp').astype(jnp.float32)]
    reduce_scatter x1, waiting for transfers between devices: 59.9 us -> 21.3 us  [per_device(): lax.psum_scatter(grad_down.astype(jnp.bfloat16), 'dp', scatter_dimension=...]
    reduce_scatter x1, waiting for transfers between devices: 0.01 us -> 35.3 us  [per_device(): lax.psum_scatter(grad_value_w.astype(jnp.bfloat16), 'dp', scatter_dimensi...]
    reduce_scatter x1, waiting for transfers between devices: 0.02 us -> 34.3 us  [per_device(): lax.psum_scatter(grad_key_w.astype(jnp.bfloat16), 'dp', scatter_dimension...]
  transfers between devices with their start and end apart: 15 -> 16, of which waited for: 11 -> 12; matrix products, arithmetic and copies ran while one was open for 12% -> 21% of each run, Pallas kernels for 0% -> 0%
where the time goes in v1:
time: 1410 us; the launch traced here: 1400 us
  waiting for transfers between devices  972 us (69%)
  matrix products  200 us (14%)
  other arithmetic  90.9 us (6%)
  local copies, waits for them, and re-layouts  63.9 us (5%)
  blocking collectives  51.5 us (4%)
  between operations  15.5 us (1%)
    all_gather x1, waiting for transfers between devices, per_device(): all_gather(mlp_partial.astype(jnp.bfloat16), 'mp')  280 us
    psum x1, waiting for transfers between devices, per_device(): lax.psum(partial_one.astype(jnp.bfloat16), 'mp').astype(jnp.float32)  155 us
    psum x1, waiting for transfers between devices, per_device(): lax.psum(attn_partial.astype(jnp.bfloat16), 'mp').astype(jnp.float32)  145 us
    psum x1, waiting for transfers between devices, per_device(): lax.psum(partial_two.astype(jnp.bfloat16), 'mp').astype(jnp.float32)  110 us
    reduce_scatter x1, waiting for transfers between devices, per_device(): lax.psum_scatter(grad_out_w.astype(jnp.bfloat16), 'dp', scatter_dimension...  42.9 us
    reduce_scatter x1, waiting for transfers between devices, per_device(): lax.psum_scatter(grad_query_w.astype(jnp.bfloat16), 'dp', scatter_dimensi...  42.5 us
    dynamic_update_slice x4, local copies, waits for them, and re-layouts, per_device(): lax.map(backward_one, (query_rot, key_rot, value_rows, doc_ids, logsum, g...  41.4 us
    reduce_scatter x1, waiting for transfers between devices, per_device(): lax.psum_scatter(grad_value_w.astype(jnp.bfloat16), 'dp', scatter_dimensi...  35.3 us
  transfers between devices with their start and end apart: 16, of which 12 were waited for; matrix products, arithmetic and copies ran while one was open for 21% of the time, Pallas kernels for 0%

profile of v1, /device:TPU:0, one launch (start us, length us, event | category | flops | bytes accessed | tf_op | source)
XLA Modules:
  0.0 1395.2 jit_solution(2791962362640767073)
XLA Ops:
  13.2 10.4 all-gather.1
  23.7 9.8 all_gather.35
  39.2 9.1 all_gather.34
  65.9 15.0 %while.26 = (s32[]{:T(128)}, bf16[2,512,512]{2,1,0:T(8,128)(2,1)S(1)}, f32[2,1,8,512,1]{3,2,4,1,0:T(8,128)}, bf16[2,512,1,64]{1,3,2,0:T(8,128)(2,1)S(1)}, s32[2,...) while((s32[]{:T(128)}, ...), condition=%wide.region_4.5_spmd, body=%wide.region_1.4_spmd.sunk | while | flops 562819072 | bytes 29630048 | solution.py:165
  98.1 144.9 %all-reduce.7.cloned.1.call-done = bf16[1024,2048]{1,0:T(8,128)(2,1)} async-done(((bf16[1024,2048]{1,0:T(8,128)(2,1)}), bf16[1024,2048]{1,0:T(8,128)(2,1)}) %all-reduce.7.cloned.1.call-update) | async-done | bytes 4194320 | tf_op jit(solution)/shard_map/psum | solution.py:168
  253.1 33.8 %all-gather.14.cloned.1.call-done = bf16[2048,1408]{1,0:T(8,128)(2,1)} async-done(((bf16[256,1408]{1,0:T(8,128)(2,1)}), bf16[2048,1408]{1,0:T(8,128)(2,1)}) %all-gather.14.cloned.1.call-update) | async-done | bytes 5767184 | tf_op jit(solution)/shard_map/all_gather | solution.py:131
  286.9 11.7 fusion.90
  298.6 33.3 %all-gather.16.cloned.1.call-done = bf16[2048,1408]{1,0:T(8,128)(2,1)} async-done(((bf16[256,1408]{1,0:T(8,128)(2,1)}), bf16[2048,1408]{1,0:T(8,128)(2,1)}) %all-gather.16.cloned.1.call-update) | async-done | bytes 5767184 | tf_op jit(solution)/shard_map/all_gather | solution.py:132
  331.9 11.7 fusion.91
  343.6 34.3 %all-gather.18.cloned.1.call-done = bf16[1408,2048]{1,0:T(8,128)(2,1)} async-done(((bf16[1408,256]{1,0:T(8,128)(2,1)}), bf16[1408,2048]{1,0:T(8,128)(2,1)}) %all-gather.18.cloned.1.call-update) | async-done | bytes 5767184 | tf_op jit(solution)/shard_map/all_gather | solution.py:133
  377.9 14.7 %multiply_convert_fusion.1 = (bf16[1024,1408]{1,0:T(8,128)(2,1)S(1)}, bf16[1024,1408]{1,0:T(8,128)(2,1)S(1)}, bf16[1024,1408]{1,0:T(8,128)(2,1)S(1)}) fusion(f32[1024,1408]{1,0:T(8,128)} %fusion.90, f32[1024,1408]{1,0:T(8,128)} %fusion.91, bf16[1408,2048]{1,0:T(8,128)(2,1)} %all-gather.18.cloned.1.call-done, bf16[1024,2048]{1,0:T(8,128)(2,1)} %param.29, ...), kind=kOutput, calls=%fused_computation.103 | convolution fusion | flops 5933498368 | bytes 30150656 | tf_op jit(solution)/shard_map/td,fd->tf/dot_general | solution.py:184
  392.6 10.9 fusion.92
  412.1 11.0 convolution_convert_fusion.3
  423.1 11.0 convolution_convert_fusion.2
  434.2 11.0 convolution_convert_fusion.1
  445.2 11.6 convolution_convert_fusion
  456.9 110.3 %all-reduce.9.cloned.1.call-done = bf16[1024,2048]{1,0:T(8,128)(2,1)} async-done(((bf16[1024,2048]{1,0:T(8,128)(2,1)}), bf16[1024,2048]{1,0:T(8,128)(2,1)}) %all-reduce.9.cloned.1.call-update) | async-done | bytes 4194320 | tf_op jit(solution)/shard_map/psum | solution.py:196
  574.2 280.3 %all-gather.20.cloned.1.call-done = bf16[4096,2048]{1,0:T(8,128)(2,1)} async-done(((bf16[1024,2048]{1,0:T(8,128)(2,1)}), bf16[4096,2048]{1,0:T(8,128)(2,1)}) %all-gather.20.cloned.1.call-update) | async-done | bytes 16777232 | tf_op jit(solution)/shard_map/all_gather | solution.py:179
  854.5 12.1 reduce_sum.86
  866.6 11.9 fusion.62
  882.4 98.6 %while.27 = (s32[]{:T(128)}, f32[2,512,8,64]{1,0,3,2:T(2,128)}, f32[2,512,1,64]{1,3,2,0:T(8,128)S(1)}, bf16[2,512,1,64]{1,3,2,0:T(8,128)(2,1)}, bf16[2,512,1,64]...) while((s32[]{:T(128)}, f32[2,512,8,64]{1,0,3,2:T(2,128)}, ...), condition=%wide.region_12.13_spmd, body=%wide.region_10.12_spmd.sunk | while | flops 1374711808 | bytes 120120048 | solution.py:211
  901.8 19.6 %dynamic_update_slice.32 = f32[2,512,8,64]{1,0,3,2:T(2,128)} dynamic-update-slice(f32[2,512,8,64]{1,0,3,2:T(2,128)} %get-tuple-element.376, f32[1,512,8,64]{1,0,3,2:T(1,128)S(1)} %copy.100, s32[]{:T(128)} %get-tuple-element.375, s32[]{:T(128)} %constant.67.clone.1..sunk, s32[]{:T(128)} %constant.67.clone.1..sunk, s32[]{:T(128)} %constant.67.clone.1..sunk) | dynamic-update-slice | bytes 2097156 | tf_op jit(solution)/shard_map/while/body/jit(dynamic_update_index_in_dim)/dynamic_update_slice | solution.py:211
  951.9 19.6 %dynamic_update_slice.32 = f32[2,512,8,64]{1,0,3,2:T(2,128)} dynamic-update-slice(f32[2,512,8,64]{1,0,3,2:T(2,128)} %get-tuple-element.376, f32[1,512,8,64]{1,0,3,2:T(1,128)S(1)} %copy.100, s32[]{:T(128)} %get-tuple-element.375, s32[]{:T(128)} %constant.67.clone.1..sunk, s32[]{:T(128)} %constant.67.clone.1..sunk, s32[]{:T(128)} %constant.67.clone.1..sunk) | dynamic-update-slice | bytes 2097156 | tf_op jit(solution)/shard_map/while/body/jit(dynamic_update_index_in_dim)/dynamic_update_slice | solution.py:211
  989.6 8.7 convolution_convert_fusion.5
  1018.6 21.3 %reduce-scatter.20.cloned.1.call-done = bf16[1408,256]{1,0:T(8,128)(2,1)} async-done(((bf16[1408,2048]{1,0:T(8,128)(2,1)}), bf16[1408,256]{1,0:T(8,128)(2,1)}) %reduce-scatter.20.cloned.1.call-update) | async-done | bytes 720912 | tf_op jit(solution)/shard_map/reduce_scatter | solution.py:271
  1042.1 34.3 %reduce-scatter.10.cloned.1.call-done = bf16[256,64]{0,1:T(8,128)(2,1)} async-done(((bf16[2048,64]{0,1:T(8,128)(2,1)}), bf16[256,64]{0,1:T(8,128)(2,1)}) %reduce-scatter.10.cloned.1.call-update) | async-done | bytes 32784 | tf_op jit(solution)/shard_map/reduce_scatter | solution.py:256
  1077.8 35.3 %reduce-scatter.12.cloned.1.call-done = bf16[256,64]{0,1:T(8,128)(2,1)} async-done(((bf16[2048,64]{0,1:T(8,128)(2,1)}), bf16[256,64]{0,1:T(8,128)(2,1)}) %reduce-scatter.12.cloned.1.call-update) | async-done | bytes 32784 | tf_op jit(solution)/shard_map/reduce_scatter | solution.py:259
  1114.6 42.9 %reduce-scatter.14.cloned.1.call-done = bf16[512,256]{1,0:T(8,128)(2,1)} async-done(((bf16[512,2048]{1,0:T(8,128)(2,1)}), bf16[512,256]{1,0:T(8,128)(2,1)}) %reduce-scatter.14.cloned.1.call-update) | async-done | bytes 262160 | tf_op jit(solution)/shard_map/reduce_scatter | solution.py:262
  1159.2 42.5 %reduce-scatter.8.cloned.1.call-done = bf16[256,512]{1,0:T(8,128)(2,1)} async-done(((bf16[2048,512]{1,0:T(8,128)(2,1)}), bf16[256,512]{1,0:T(8,128)(2,1)}) %reduce-scatter.8.cloned.1.call-update) | async-done | bytes 262160 | tf_op jit(solution)/shard_map/reduce_scatter | solution.py:253
  1203.6 155.4 %all-reduce.11.cloned.1.call-done = bf16[1024,2048]{1,0:T(8,128)(2,1)} async-done(((bf16[1024,2048]{1,0:T(8,128)(2,1)}), bf16[1024,2048]{1,0:T(8,128)(2,1)}) %all-reduce.11.cloned.1.call-update) | async-done | bytes 4194320 | tf_op jit(solution)/shard_map/psum | solution.py:239
  1364.6 13.7 all-reduce.2
  1379.0 9.5 fusion.60
  (232 shorter events, 192.7 us)
Async XLA Ops:
  7.2 45.8 %all-gather.10.cloned.1.call-start = ((), (), s32[]{:S(2)}) async-start(), calls=%async_computation.7 | async-start | bytes 2359296 | tf_op jit(solution)/shard_map/all_gather | solution.py:127
  7.9 73.1 %all-gather.12.cloned.1.call-start = ((), (), s32[]{:S(2)}) async-start(), calls=%async_computation.8 | async-start | bytes 2359296 | tf_op jit(solution)/shard_map/all_gather | solution.py:130
  8.7 234.3 %all-reduce.7.cloned.1.call-start = ((), (), s32[]{:S(2)}) async-start(), calls=%async_computation.9 | async-start | bytes 8388608 | tf_op jit(solution)/shard_map/psum | solution.py:168
  8.7 24.8 %copy-start.1 = (bf16[1024,2048]{1,0:T(8,128)(2,1)S(1)}, bf16[1024,2048]{1,0:T(8,128)(2,1)}, u32[]{:S(2)}) copy-start(bf16[1024,2048]{1,0:T(8,128)(2,1)} %param.17) | copy-start | bytes 12582916
  12.6 21.9 %copy-start.26 = (f32[1024]{0:T(1024)}, f32[1024]{0:T(1024)S(1)}, u32[]{:S(2)}) copy-start(f32[1024]{0:T(1024)S(1)} %get-tuple-element.219) | copy-start | bytes 12292
  23.7 10.9 copy-start.24
  39.2 24.0 %copy-start.17 = (f32[512,32]{0,1:T(8,128)}, f32[512,32]{0,1:T(8,128)S(1)}, u32[]{:S(2)}) copy-start(f32[512,32]{0,1:T(8,128)S(1)} %get-tuple-element.224) | copy-start | bytes 196612
  87.8 10.3 copy-start.31
  87.8 199.1 %all-gather.14.cloned.1.call-start = ((), (), s32[]{:S(2)}) async-start(), calls=%async_computation.10 | async-start | bytes 6488064 | tf_op jit(solution)/shard_map/all_gather | solution.py:131
  88.4 243.5 %all-gather.16.cloned.1.call-start = ((), (), s32[]{:S(2)}) async-start(), calls=%async_computation.11 | async-start | bytes 6488064 | tf_op jit(solution)/shard_map/all_gather | solution.py:132
  89.0 288.9 %all-gather.18.cloned.1.call-start = ((), (), s32[]{:S(2)}) async-start(), calls=%async_computation.12 | async-start | bytes 6488064 | tf_op jit(solution)/shard_map/all_gather | solution.py:133
  89.5 477.6 %all-reduce.9.cloned.1.call-start = ((), (), s32[]{:S(2)}) async-start(), calls=%async_computation.13 | async-start | bytes 8388608 | tf_op jit(solution)/shard_map/psum | solution.py:196
  392.6 10.9 copy-start.37
  392.6 10.9 copy-start.38
  392.6 10.9 copy-start.32
  412.0 442.5 %all-gather.20.cloned.1.call-start = ((), (), s32[]{:S(2)}) async-start(), calls=%async_computation.22 | async-start | bytes 20971520 | tf_op jit(solution)/shard_map/all_gather | solution.py:179
  423.1 590.9 %reduce-scatter.16.cloned.1.call-start = ((), (), s32[]{:S(2)}) async-start(), calls=%async_computation.19 | async-start | bytes 6488064 | tf_op jit(solution)/shard_map/reduce_scatter | solution.py:265
  434.1 582.1 %reduce-scatter.18.cloned.1.call-start = ((), (), s32[]{:S(2)}) async-start(), calls=%async_computation.20 | async-start | bytes 6488064 | tf_op jit(solution)/shard_map/reduce_scatter | solution.py:268
  445.2 594.7 %reduce-scatter.20.cloned.1.call-start = ((), (), s32[]{:S(2)}) async-start(), calls=%async_computation.21 | async-start | bytes 6488064 | tf_op jit(solution)/shard_map/reduce_scatter | solution.py:271
  456.8 619.6 %reduce-scatter.10.cloned.1.call-start = ((), (), s32[]{:S(2)}) async-start(), calls=%async_computation.16 | async-start | bytes 294912 | tf_op jit(solution)/shard_map/reduce_scatter | solution.py:256
  866.6 11.9 copy-start.34
  882.4 98.6 %copy-start.18 = (f32[512,32]{0,1:T(8,128)S(1)}, f32[512,32]{0,1:T(8,128)}, u32[]{:S(2)}) copy-start(f32[512,32]{0,1:T(8,128)} %copy-done.17) | copy-start | bytes 196612
  882.4 98.6 %copy-start.22 = (f32[512,32]{0,1:T(8,128)S(1)}, f32[512,32]{0,1:T(8,128)}, u32[]{:S(2)}) copy-start(f32[512,32]{0,1:T(8,128)} %get-tuple-element.222) | copy-start | bytes 196612
  985.0 128.1 %reduce-scatter.12.cloned.1.call-start = ((), (), s32[]{:S(2)}) async-start(), calls=%async_computation.17 | async-start | bytes 294912 | tf_op jit(solution)/shard_map/reduce_scatter | solution.py:259
  989.5 9.1 copy-start.16
  989.5 168.0 %reduce-scatter.14.cloned.1.call-start = ((), (), s32[]{:S(2)}) async-start(), calls=%async_computation.18 | async-start | bytes 2359296 | tf_op jit(solution)/shard_map/reduce_scatter | solution.py:262
  998.3 203.4 %reduce-scatter.8.cloned.1.call-start = ((), (), s32[]{:S(2)}) async-start(), calls=%async_computation.15 | async-start | bytes 2359296 | tf_op jit(solution)/shard_map/reduce_scatter | solution.py:253
  1005.3 353.7 %all-reduce.11.cloned.1.call-start = ((), (), s32[]{:S(2)}) async-start(), calls=%async_computation.14 | async-start | bytes 8388608 | tf_op jit(solution)/shard_map/psum | solution.py:239
  1012.6 346.4 %copy-start.25 = (f32[8,1,256]{2,1,0:T(1,128)S(1)}, f32[8,1,256]{2,1,0:T(1,128)}, u32[]{:S(2)}) copy-start(f32[8,1,256]{2,1,0:T(1,128)} %copy-done.24) | copy-start | bytes 24580
  1012.6 346.4 %copy-start.27 = (f32[1024]{0:T(1024)S(1)}, f32[1024]{0:T(1024)}, u32[]{:S(2)}) copy-start(f32[1024]{0:T(1024)} %copy-done.26) | copy-start | bytes 12292
  1018.6 346.1 %copy-start.30 = (bf16[2048]{0:T(1024)(128)(2,1)S(1)}, bf16[2048]{0:T(1024)(128)(2,1)}, u32[]{:S(2)}) copy-start(bf16[2048]{0:T(1024)(128)(2,1)} %get-tuple-element.159) | copy-start | bytes 12292
  1018.6 360.4 %copy-start.29 = (f32[1024]{0:T(1024)S(1)}, f32[1024]{0:T(1024)}, u32[]{:S(2)}) copy-start(f32[1024]{0:T(1024)} %get-tuple-element.218) | copy-start | bytes 12292
  (29 other events, 123.2 us)
Sparse Core Ops, SparseCore 0:
  9.9 30.4 all-gather.9
  42.3 28.0 all-gather.11
  87.9 155.0 all-reduce.6
  244.7 42.1 all-gather.13
  288.7 43.1 all-gather.15
  333.6 44.2 all-gather.17
  412.1 154.9 all-reduce.8
  568.7 285.7 all-gather.19
  857.9 57.1 reduce-scatter.15
  918.5 58.9 reduce-scatter.17
  980.9 58.8 reduce-scatter.19
  1042.7 33.6 reduce-scatter.9
  1079.5 33.6 reduce-scatter.11
  1116.3 41.1 reduce-scatter.13
  1160.6 41.1 reduce-scatter.7
  1204.0 154.9 all-reduce.10
